TPU v7x, 32 devices: a whole 2x2x4 slice. The times are simulated.
32 devices in a mesh: row: 8 (over y, x, core), col: 4 (over z).
Axes of the slice: x: 2, y: 2, z: 4, core: 2. Of those that a mesh axis runs over, the one named last changes fastest.
Arguments:
- tokens: bfloat16 [6144, 2048], P('row', 'col'), may hold values from -6 to 6
- out_grad: bfloat16 [6144, 2048], P('row', 'col'), may hold values from -768 to 768
- counts: int32 [8], P('row'), may hold values from 65 to 768
- block_moves: int32 [4, 3], replicated, may hold values from 0 to 7, as said below
- segment_ids: int32 [6144], P('row'), may hold values from 0 to 191, never falling along the last dimension, each value on 1 to 128 neighbouring positions
- gate_weight: bfloat16 [2048, 8192], P('row', 'col'), may hold values from -0.125 to 0.125
- up_weight: bfloat16 [2048, 8192], P('row', 'col'), may hold values from -0.125 to 0.125
- down_weight: bfloat16 [2048, 8192], P('row', 'col'), may hold values from -0.0625 to 0.0625
Outputs:
- hidden: bfloat16 [4096, 8192], P('row', 'col')
- gate_grad: float32 [2048, 8192], P('row', 'col')
- up_grad: float32 [2048, 8192], P('row', 'col')
- down_grad: float32 [2048, 8192], P('row', 'col')
Inputs may be any that keep to these rules, and one draw needn't show every extreme that they name: `block_moves`: each row is (source rank, destination rank, block index); the block is a valid block of its source; no two rows share both source and destination, nor both source and block; a rank is the source of at most two rows or the destination of at most one, never both; after the moves every rank holds at most 4 valid blocks and some hold exactly 4. `segment_ids`: never falling along the whole array; each document covers 1 to 128 consecutive slots.
All inputs are finite; a program needn't handle non-finite values.
Results may differ from a plain program's by a relative error of at most 0.015.
Values may be sent and summed in bfloat16 or wider, within the bound.
A program may use at most 128 MiB of HBM per device.

v0:
```python
import jax
import jax.numpy as jnp
from jax import lax
from jax.sharding import PartitionSpec as P

BLOCK = 128
WORK = 4


def local_terms(gate_sum, up_sum, back_sum):
    logistic = jax.nn.sigmoid(gate_sum)
    activated = gate_sum * logistic
    hidden = (activated * up_sum).astype(jnp.bfloat16)
    gate_back = (back_sum * up_sum * logistic * (1.0 + gate_sum * (1.0 - logistic))).astype(
        jnp.bfloat16
    )
    up_back = (back_sum * activated).astype(jnp.bfloat16)
    return (hidden, gate_back, up_back)


def contract(left_side, right_side):
    return lax.dot_general(
        left_side, right_side, (((0,), (0,)), ((), ())), preferred_element_type=jnp.float32
    )


def on_device(
    tokens, out_grad, counts, block_moves, segment_ids, gate_weight, up_weight, down_weight
):
    ranks_all = lax.axis_size("row")
    me_rank = lax.axis_index("row")
    slot_rows = tokens.shape[0]
    cap_blocks = slot_rows // BLOCK
    feat_cols = tokens.shape[1]
    my_count = counts[0]
    places = jnp.arange(slot_rows, dtype=jnp.int32)
    following = jnp.concatenate([segment_ids[1:], segment_ids[-1:]])
    own_weight = ((places + 1 < my_count) & (following == segment_ids)).astype(jnp.float32)
    source = block_moves[:, 0]
    target = block_moves[:, 1]
    block_id = block_moves[:, 2]
    block_ids = jnp.arange(cap_blocks, dtype=jnp.int32)
    filled = (my_count + BLOCK - 1) // BLOCK
    moved_out = jnp.any(
        (source[None, :] == me_rank) & (block_id[None, :] == block_ids[:, None]), axis=1
    )
    kept_flag = (block_ids < filled) & jnp.logical_not(moved_out)
    arrive = target == me_rank
    flag_bits = jnp.concatenate([kept_flag, arrive]).astype(jnp.int32)
    local_ids = jnp.concatenate([block_ids, cap_blocks + source])
    list_place = jnp.cumsum(flag_bits) - 1
    slot_ids = jnp.arange(WORK, dtype=jnp.int32)
    slot_hit = (flag_bits[:, None] == 1) & (list_place[:, None] == slot_ids[None, :])
    slot_index = jnp.sum(jnp.where(slot_hit, local_ids[:, None] + 1, 0), axis=0) - 1
    peer_ids = jnp.arange(ranks_all, dtype=jnp.int32)
    outgoing = (source[None, :] == me_rank) & (target[None, :] == peer_ids[:, None])
    send_block = jnp.sum(jnp.where(outgoing, block_id[None, :], 0), axis=1)
    send_live = jnp.any(outgoing, axis=1)
    own_tokens = tokens.reshape(cap_blocks, BLOCK, feat_cols)
    own_grad = out_grad.reshape(cap_blocks, BLOCK, feat_cols)
    own_mask = own_weight.astype(jnp.bfloat16).reshape(cap_blocks, BLOCK)

    def outbox(block_rows):
        chosen = jnp.take(block_rows, send_block, axis=0)
        live_rows = send_live.reshape((-1,) + (1,) * (chosen.ndim - 1))
        return jnp.where(live_rows, chosen, jnp.zeros_like(chosen))

    whole_count = jnp.sum(own_weight).astype(jnp.int32)
    count_parts = jnp.broadcast_to(
        jnp.stack([whole_count // 256, whole_count % 256]).astype(jnp.bfloat16)[None, :],
        (ranks_all, 2),
    )
    got_tokens, got_grad, got_mask, got_parts = (
        lax.all_to_all(outbox(own_tokens), "row", split_axis=0, concat_axis=0, tiled=True),
        lax.all_to_all(outbox(own_grad), "row", split_axis=0, concat_axis=0, tiled=True),
        lax.all_to_all(outbox(own_mask), "row", split_axis=0, concat_axis=0, tiled=True),
        lax.all_to_all(count_parts, "row", split_axis=0, concat_axis=0, tiled=True),
    )
    part_values = got_parts.astype(jnp.float32)
    loss_total = 256.0 * jnp.sum(part_values[:, 0]) + jnp.sum(part_values[:, 1])

    def to_work(pool_rows):
        chosen = jnp.take(pool_rows, jnp.maximum(slot_index, 0), axis=0)
        live_rows = (slot_index >= 0).reshape((-1,) + (1,) * (chosen.ndim - 1))
        return jnp.where(live_rows, chosen, jnp.zeros_like(chosen))

    work_tokens = to_work(jnp.concatenate([own_tokens, got_tokens])).reshape(
        WORK * BLOCK, feat_cols
    )
    work_grad = to_work(jnp.concatenate([own_grad, got_grad])).reshape(WORK * BLOCK, feat_cols)
    work_mask = to_work(jnp.concatenate([own_mask, got_mask])).reshape(WORK * BLOCK)
    work_weight = work_mask.astype(jnp.float32)
    full_tokens, full_grad = (
        lax.all_gather(work_tokens, "col", axis=1, tiled=True),
        lax.all_gather(work_grad, "col", axis=1, tiled=True),
    )
    hidden_cols = gate_weight.shape[1]
    gate_piece = lax.all_gather(gate_weight, "row", axis=0, tiled=True)
    up_piece = lax.all_gather(up_weight, "row", axis=0, tiled=True)
    down_piece = lax.all_gather(down_weight, "row", axis=0, tiled=True)
    gate_sum = jnp.dot(full_tokens, gate_piece, preferred_element_type=jnp.float32)
    up_sum = jnp.dot(full_tokens, up_piece, preferred_element_type=jnp.float32)
    back_raw = jnp.dot(full_grad, down_piece, preferred_element_type=jnp.float32)
    back_sum = back_raw * work_weight[:, None]
    hidden, gate_back, up_back = local_terms(gate_sum, up_sum, back_sum)
    weighted = full_grad * work_mask[:, None]

    def term_rows(left_side, right_side):
        return contract(left_side, right_side) / loss_total

    down_grad = lax.psum_scatter(
        term_rows(weighted, hidden).astype(jnp.bfloat16), "row", scatter_dimension=0, tiled=True
    ).astype(jnp.float32)
    other_part = lax.psum_scatter(
        jnp.concatenate(
            [term_rows(full_tokens, gate_back), term_rows(full_tokens, up_back)], axis=1
        ).astype(jnp.bfloat16),
        "row",
        scatter_dimension=0,
        tiled=True,
    ).astype(jnp.float32)
    gate_grad = other_part[:, :hidden_cols]
    up_grad = other_part[:, hidden_cols:]
    return (hidden, gate_grad, up_grad, down_grad)


def solution(mesh):
    placed = (
        P("row", "col"),
        P("row", "col"),
        P("row"),
        P(),
        P("row"),
        P("row", "col"),
        P("row", "col"),
        P("row", "col"),
    )
    return jax.shard_map(
        on_device,
        mesh=mesh,
        in_specs=placed,
        out_specs=(P("row", "col"), P("row", "col"), P("row", "col"), P("row", "col")),
        check_vma=False,
    )
```

profile of v0, /device:TPU:0, one launch (start us, length us, event | category | flops | bytes accessed | tf_op | source)
XLA Modules:
  0.0 525.0 jit_solution(14892905460877287616)
XLA Ops:
  13.7 5.3 %all-to-all-start = ((bf16[8,128,512]{2,1,0:T(8,128)(2,1)}), bf16[8,128,512]{2,1,0:T(8,128)(2,1)S(1)}, u32[]{:S(2)}, u32[]{:S(2)}) async-start(bf16[8,128,512]{2,1,0:T(8,128)(2,1)} %get-tuple-element.40), calls=%async_computation | async-start | bytes 2097152 | tf_op jit(solution)/shard_map/all_to_all | solution.py:74
  20.2 14.2 %all-to-all-done = bf16[8,128,512]{2,1,0:T(8,128)(2,1)S(1)} async-done(((bf16[8,128,512]{2,1,0:T(8,128)(2,1)}), bf16[8,128,512]{2,1,0:T(8,128)(2,1)S(1)}, u32[]{:S(2)}, u32[]{:S(2)}) %all-to-all-start) | async-done | bytes 1048608 | tf_op jit(solution)/shard_map/all_to_all | solution.py:74
  34.4 4.2 all-to-all-start.1
  42.4 11.6 %all-to-all-done.1 = bf16[8,128,512]{2,1,0:T(8,128)(2,1)} async-done(((bf16[8,128,512]{2,1,0:T(8,128)(2,1)}), bf16[8,128,512]{2,1,0:T(8,128)(2,1)}, u32[]{:S(2)}, u32[]{:S(2)}) %all-to-all-start.1) | async-done | bytes 1048608 | tf_op jit(solution)/shard_map/all_to_all | solution.py:75
  63.2 3.3 all-to-all-start.3
  67.8 3.3 all-to-all-done.3
  71.1 3.3 all-to-all-start.2
  79.6 22.8 %all-gather.6.cloned.1.call-done = bf16[512,2048]{1,0:T(8,128)(2,1)} async-done(((bf16[512,512]{1,0:T(8,128)(2,1)}), bf16[512,2048]{1,0:T(8,128)(2,1)}) %all-gather.6.cloned.1.call-update) | async-done | bytes 2097168 | tf_op jit(solution)/shard_map/all_gather | solution.py:94
  102.4 55.0 %all-gather.8.cloned.1.call-done = bf16[2048,2048]{1,0:T(8,128)(2,1)} async-done(((bf16[256,2048]{1,0:T(8,128)(2,1)}), bf16[2048,2048]{1,0:T(8,128)(2,1)}) %all-gather.8.cloned.1.call-update) | async-done | bytes 8388624 | tf_op jit(solution)/shard_map/all_gather | solution.py:98
  157.4 10.5 %fusion.23 = f32[512,2048]{1,0:T(8,128)} fusion(bf16[512,2048]{1,0:T(8,128)(2,1)} %all-gather.6.cloned.1.call-done, bf16[2048,2048]{1,0:T(8,128)(2,1)} %all-gather.8.cloned.1.call-done), kind=kOutput, calls=%fused_computation.76 | convolution fusion | flops 4294967296 | bytes 14680064 | tf_op jit(solution)/shard_map/dot_general | solution.py:101
  167.9 45.7 %all-gather.10.cloned.1.call-done = bf16[2048,2048]{1,0:T(8,128)(2,1)} async-done(((bf16[256,2048]{1,0:T(8,128)(2,1)}), bf16[2048,2048]{1,0:T(8,128)(2,1)}) %all-gather.10.cloned.1.call-update) | async-done | bytes 8388624 | tf_op jit(solution)/shard_map/all_gather | solution.py:99
  213.6 10.9 %multiply_convert_fusion.2 = (bf16[512,2048]{1,0:T(8,128)(2,1)}, f32[512,2048]{1,0:T(8,128)}) fusion(f32[512,2048]{1,0:T(8,128)} %fusion.23, bf16[512,2048]{1,0:T(8,128)(2,1)S(1)} %copy-done.3, bf16[2048,2048]{1,0:T(8,128)(2,1)} %all-gather.10.cloned.1.call-done), kind=kOutput, calls=%fused_computation.12 | convolution fusion | flops 4301258752 | bytes 20971520 | tf_op jit(solution)/shard_map/dot_general | solution.py:102
  224.5 36.8 %all-gather.12.cloned.1.call-done = bf16[512,2048]{1,0:T(8,128)(2,1)} async-done(((bf16[512,512]{1,0:T(8,128)(2,1)}), bf16[512,2048]{1,0:T(8,128)(2,1)}) %all-gather.12.cloned.1.call-update) | async-done | bytes 2097168 | tf_op jit(solution)/shard_map/all_gather | solution.py:95
  261.3 10.5 %divide_convert_fusion = bf16[2048,2048]{0,1:T(8,128)(2,1)} fusion(f32[]{:T(128)S(6)} %add.97, bf16[512,2048]{1,0:T(8,128)(2,1)} %get-tuple-element.43, bf16[512,2048]{1,0:T(8,128)(2,1)} %all-gather.12.cloned.1.call-done, bf16[512]{0:T(512)(128)(2,1)S(1)} %get-tuple-element.29), kind=kOutput, calls=%fused_computation.7 | convolution fusion | flops 4304404480 | bytes 12583940 | tf_op jit(solution)/shard_map/dot_general | solution.py:22
  272.0 44.1 %all-gather.14.cloned.1.call-done = bf16[2048,2048]{1,0:T(8,128)(2,1)} async-done(((bf16[256,2048]{1,0:T(8,128)(2,1)}), bf16[2048,2048]{1,0:T(8,128)(2,1)}) %all-gather.14.cloned.1.call-update) | async-done | bytes 8388624 | tf_op jit(solution)/shard_map/all_gather | solution.py:100
  316.1 7.7 %fusion.24 = f32[512,2048]{1,0:T(8,128)S(1)} fusion(bf16[512,2048]{1,0:T(8,128)(2,1)} %all-gather.12.cloned.1.call-done, bf16[2048,2048]{1,0:T(8,128)(2,1)} %all-gather.14.cloned.1.call-done), kind=kOutput, calls=%fused_computation.77 | convolution fusion | flops 4294967296 | bytes 14680064 | tf_op jit(solution)/shard_map/dot_general | solution.py:103
  325.9 8.0 %divide_convert_fusion.2 = bf16[2048,2048]{0,1:T(8,128)(2,1)S(1)} fusion(f32[]{:T(128)S(6)} %add.97, bf16[512,2048]{1,0:T(8,128)(2,1)S(1)} %copy-done.3, f32[512,2048]{1,0:T(8,128)S(1)} %copy-done.4, f32[512,2048]{1,0:T(8,128)} %get-tuple-element.44, f32[512,2048]{1,0:T(8,128)S(1)} %fusion.24, f32[512]{0:T(512)S(1)} %get-tuple-element.28), kind=kOutput, calls=%fused_computation.9 | convolution fusion | flops 4314890240 | bytes 23070724 | tf_op jit(solution)/shard_map/dot_general | solution.py:22
  333.8 10.9 %divide_convert_fusion.1 = bf16[2048,2048]{0,1:T(8,128)(2,1)} fusion(f32[]{:T(128)S(6)} %add.97, bf16[512,2048]{1,0:T(8,128)(2,1)S(1)} %copy-done.3, f32[512,2048]{1,0:T(8,128)} %copy-done.5, f32[512]{0:T(512)S(1)} %get-tuple-element.28, f32[512,2048]{1,0:T(8,128)S(1)} %copy-done.4), kind=kOutput, calls=%fused_computation.8 | convolution fusion | flops 4310695936 | bytes 18876420 | tf_op jit(solution)/shard_map/dot_general | solution.py:22
  344.7 10.8 %pad_maximum_fusion = bf16[2048,4096]{0,1:T(8,128)(2,1)} fusion(bf16[2048,2048]{0,1:T(8,128)(2,1)} %divide_convert_fusion.1, bf16[2048,2048]{0,1:T(8,128)(2,1)S(1)} %divide_convert_fusion.2), kind=kLoop, calls=%fused_computation.6 | loop fusion | flops 33554432 | bytes 33554432 | tf_op jit(solution)/shard_map/concatenate | solution.py:115
  355.5 35.2 %reduce-scatter.5.cloned.1.call-done = bf16[256,2048]{0,1:T(8,128)(2,1)} async-done(((bf16[2048,2048]{0,1:T(8,128)(2,1)}), bf16[256,2048]{0,1:T(8,128)(2,1)}) %reduce-scatter.5.cloned.1.call-update) | async-done | bytes 1048592 | tf_op jit(solution)/shard_map/reduce_scatter | solution.py:111
  390.7 2.6 copy.49
  393.3 117.0 %reduce-scatter.3.cloned.1.call-done = bf16[256,4096]{0,1:T(8,128)(2,1)} async-done(((bf16[2048,4096]{0,1:T(8,128)(2,1)}), bf16[256,4096]{0,1:T(8,128)(2,1)}) %reduce-scatter.3.cloned.1.call-update) | async-done | bytes 2097168 | tf_op jit(solution)/shard_map/reduce_scatter | solution.py:114
  510.3 3.2 fusion.21
  513.5 2.9 copy.48
  (79 shorter events, 28.5 us)
Async XLA Ops:
  12.1 26.9 %copy-start = (bf16[768,512]{1,0:T(8,128)(2,1)S(1)}, bf16[768,512]{1,0:T(8,128)(2,1)}, u32[]{:S(2)}) copy-start(bf16[768,512]{1,0:T(8,128)(2,1)} %param.12) | copy-start | bytes 2359300
  13.7 40.3 %copy-start.1 = (bf16[768,512]{1,0:T(8,128)(2,1)S(1)}, bf16[768,512]{1,0:T(8,128)(2,1)}, u32[]{:S(2)}) copy-start(bf16[768,512]{1,0:T(8,128)(2,1)} %param.13) | copy-start | bytes 2359300
  13.7 20.7 %all-to-all-start = ((bf16[8,128,512]{2,1,0:T(8,128)(2,1)}), bf16[8,128,512]{2,1,0:T(8,128)(2,1)S(1)}, u32[]{:S(2)}, u32[]{:S(2)}) async-start(bf16[8,128,512]{2,1,0:T(8,128)(2,1)} %get-tuple-element.40), calls=%async_computation | async-start | bytes 2097152 | tf_op jit(solution)/shard_map/all_to_all | solution.py:74
  34.4 19.6 %all-to-all-start.1 = ((bf16[8,128,512]{2,1,0:T(8,128)(2,1)}), bf16[8,128,512]{2,1,0:T(8,128)(2,1)}, u32[]{:S(2)}, u32[]{:S(2)}) async-start(bf16[8,128,512]{2,1,0:T(8,128)(2,1)} %get-tuple-element.39), calls=%async_computation.1 | async-start | bytes 2097152 | tf_op jit(solution)/shard_map/all_to_all | solution.py:75
  38.6 63.8 %all-gather.6.cloned.1.call-start = ((), (), s32[]{:S(2)}) async-start(), calls=%async_computation.6 | async-start | bytes 2621440 | tf_op jit(solution)/shard_map/all_gather | solution.py:94
  55.4 4.4 copy-start.2
  57.2 100.2 %all-gather.8.cloned.1.call-start = ((), (), s32[]{:S(2)}) async-start(), calls=%async_computation.7 | async-start | bytes 9437184 | tf_op jit(solution)/shard_map/all_gather | solution.py:98
  58.0 155.6 %all-gather.10.cloned.1.call-start = ((), (), s32[]{:S(2)}) async-start(), calls=%async_computation.8 | async-start | bytes 9437184 | tf_op jit(solution)/shard_map/all_gather | solution.py:99
  58.7 202.6 %all-gather.12.cloned.1.call-start = ((), (), s32[]{:S(2)}) async-start(), calls=%async_computation.9 | async-start | bytes 2621440 | tf_op jit(solution)/shard_map/all_gather | solution.py:95
  59.3 256.8 %all-gather.14.cloned.1.call-start = ((), (), s32[]{:S(2)}) async-start(), calls=%async_computation.10 | async-start | bytes 9437184 | tf_op jit(solution)/shard_map/all_gather | solution.py:100
  63.2 7.9 %all-to-all-start.3 = ((bf16[8,1,2]{2,1,0:T(2,128)(2,1)}), bf16[8,1,2]{2,1,0:T(2,128)(2,1)S(1)}, u32[]{:S(2)}, u32[]{:S(2)}) async-start(bf16[8,1,2]{2,1,0:T(2,128)(2,1)} %broadcast_in_dim.133), calls=%async_computation.3 | async-start | bytes 8192 | tf_op jit(solution)/shard_map/all_to_all | solution.py:77
  71.1 7.9 %all-to-all-start.2 = ((bf16[8,1,128]{2,1,0:T(2,128)(2,1)}), bf16[8,1,128]{2,1,0:T(2,128)(2,1)S(1)}, u32[]{:S(2)}, u32[]{:S(2)}) async-start(bf16[8,1,128]{2,1,0:T(2,128)(2,1)} %copy.44), calls=%async_computation.2 | async-start | bytes 8192 | tf_op jit(solution)/shard_map/all_to_all | solution.py:76
  74.4 316.3 %reduce-scatter.5.cloned.1.call-start = ((), (), s32[]{:S(2)}) async-start(), calls=%async_computation.12 | async-start | bytes 9437184 | tf_op jit(solution)/shard_map/reduce_scatter | solution.py:111
  102.4 111.2 %copy-start.3 = (bf16[512,2048]{1,0:T(8,128)(2,1)S(1)}, bf16[512,2048]{1,0:T(8,128)(2,1)}, u32[]{:S(2)}) copy-start(bf16[512,2048]{1,0:T(8,128)(2,1)} %all-gather.6.cloned.1.call-done) | copy-start | bytes 6291460
  271.7 238.6 %reduce-scatter.3.cloned.1.call-start = ((), (), s32[]{:S(2)}) async-start(), calls=%async_computation.11 | async-start | bytes 18874368 | tf_op jit(solution)/shard_map/reduce_scatter | solution.py:114
  316.1 9.8 %copy-start.4 = (f32[512,2048]{1,0:T(8,128)S(1)}, f32[512,2048]{1,0:T(8,128)}, u32[]{:S(2)}) copy-start(f32[512,2048]{1,0:T(8,128)} %fusion.23) | copy-start | bytes 12582916
  323.8 2.1 copy-start.5
Sparse Core Ops, SparseCore 0:
  57.3 45.0 all-gather.5
  104.3 53.0 all-gather.7
  159.3 54.2 all-gather.9
  215.6 45.6 all-gather.11
  263.0 53.0 all-gather.13
  319.4 71.2 reduce-scatter.4
  394.3 115.9 reduce-scatter.2
where the time goes:
time: 526 us; the launch traced here: 525 us
  waiting for transfers between devices  391 us (74%)
  matrix products  58.4 us (11%)
  local copies, waits for them, and re-layouts  22.9 us (4%)
  other arithmetic  19.4 us (4%)
  starting transfers between devices  16.9 us (3%)
  between operations  16.9 us (3%)
    reduce_scatter x1, waiting for transfers between devices, on_device(): lax.psum_scatter(jnp.concatenate([term_rows(full_tokens, gate_back), term...  117 us
    all_gather x1, waiting for transfers between devices, on_device(): gate_piece = lax.all_gather(gate_weight, 'row', axis=0, tiled=True)  55 us
    all_gather x1, waiting for transfers between devices, on_device(): up_piece = lax.all_gather(up_weight, 'row', axis=0, tiled=True)  45.7 us
    all_gather x1, waiting for transfers between devices, on_device(): down_piece = lax.all_gather(down_weight, 'row', axis=0, tiled=True)  44.1 us
    all_gather x1, waiting for transfers between devices, on_device(): lax.all_gather(work_grad, 'col', axis=1, tiled=True)  36.8 us
    reduce_scatter x1, waiting for transfers between devices, on_device(): lax.psum_scatter(term_rows(weighted, hidden).astype(jnp.bfloat16), 'row',...  35.2 us
    dot_general x3, matrix products, contract(): lax.dot_general(left_side, right_side, (((0,), (0,)), ((), ())), preferre...  29.3 us
    all_gather x1, waiting for transfers between devices, on_device(): lax.all_gather(work_tokens, 'col', axis=1, tiled=True)  22.8 us
  transfers between devices with their start and end apart: 11, of which 11 were waited for; matrix products, arithmetic and copies ran while one was open for 15% of the time, Pallas kernels for 0%

commit v1 on v0

--- a/solution.py
+++ b/solution.py
@@ -97,7 +97,12 @@
     hidden_cols = gate_weight.shape[1]
     gate_piece = lax.all_gather(gate_weight, "row", axis=0, tiled=True)
     up_piece = lax.all_gather(up_weight, "row", axis=0, tiled=True)
-    down_piece = lax.all_gather(down_weight, "row", axis=0, tiled=True)
+    ring = [down_weight]
+    for hop in range(7):
+        ring.append(lax.ppermute(ring[-1], "row", [(dev, (dev + 1) % 8) for dev in range(8)]))
+    down_piece = jnp.roll(
+        jnp.concatenate(ring[::-1], axis=0), (lax.axis_index("row") + 1) * ring[0].shape[0], axis=0
+    )
     gate_sum = jnp.dot(full_tokens, gate_piece, preferred_element_type=jnp.float32)
     up_sum = jnp.dot(full_tokens, up_piece, preferred_element_type=jnp.float32)
     back_raw = jnp.dot(full_grad, down_piece, preferred_element_type=jnp.float32)

time: 526 us -> 500 us (0.951)
  waiting for transfers between devices: 391 us -> 344 us
  local copies, waits for them, and re-layouts: 22.9 us -> 37.8 us
    ppermute x0 -> x7, waiting for transfers between devices: none -> 97.5 us  [on_device(): lax.ppermute(ring[-1], 'row', [(dev, (dev + 1) % 8) for dev in range(8)])]
    all_gather x1, waiting for transfers between devices: 55 us -> 0.01 us  [on_device(): gate_piece = lax.all_gather(gate_weight, 'row', axis=0, tiled=True)]
    all_gather x1 -> x0, waiting for transfers between devices: 44.1 us -> none  [on_device(): down_piece = lax.all_gather(down_weight, 'row', axis=0, tiled=True)]
    all_gather x1, waiting for transfers between devices: 22.8 us -> 0.01 us  [on_device(): lax.all_gather(work_tokens, 'col', axis=1, tiled=True)]
    reduce_scatter x1, waiting for transfers between devices: 35.2 us -> 18.8 us  [on_device(): lax.psum_scatter(term_rows(weighted, hidden).astype(jnp.bfloat16), 'row',...]
    unnamed x18 -> x41, local copies, waits for them, and re-layouts: 9.54 us -> 22.8 us
    all_to_all x1, waiting for transfers between devices: 2.38 us -> 9.2 us  [on_device(): lax.all_to_all(outbox(own_mask), 'row', split_axis=0, concat_axis=0, tile...]
    all_gather x1, waiting for transfers between devices: 45.7 us -> 39.9 us  [on_device(): up_piece = lax.all_gather(up_weight, 'row', axis=0, tiled=True)]
  transfers between devices with their start and end apart: 11 -> 17, of which waited for: 11 -> 12; matrix products, arithmetic and copies ran while one was open for 15% -> 19% of each run, Pallas kernels for 0% -> 0%
where the time goes in v1:
time: 500 us; the launch traced here: 498 us
  waiting for transfers between devices  344 us (69%)
  matrix products  60.4 us (12%)
  local copies, waits for them, and re-layouts  37.8 us (8%)
  other arithmetic  20.5 us (4%)
  starting transfers between devices  18.2 us (4%)
  between operations  17 us (3%)
    reduce_scatter x1, waiting for transfers between devices, on_device(): lax.psum_scatter(jnp.concatenate([term_rows(full_tokens, gate_back), term...  117 us
    ppermute x7, waiting for transfers between devices, on_device(): lax.ppermute(ring[-1], 'row', [(dev, (dev + 1) % 8) for dev in range(8)])  97.5 us
    all_gather x1, waiting for transfers between devices, on_device(): up_piece = lax.all_gather(up_weight, 'row', axis=0, tiled=True)  39.9 us
    all_gather x1, waiting for transfers between devices, on_device(): lax.all_gather(work_grad, 'col', axis=1, tiled=True)  35 us
    dot_general x3, matrix products, contract(): lax.dot_general(left_side, right_side, (((0,), (0,)), ((), ())), preferre...  30.8 us
    unnamed x41, local copies, waits for them, and re-layouts  22.8 us
    reduce_scatter x1, waiting for transfers between devices, on_device(): lax.psum_scatter(term_rows(weighted, hidden).astype(jnp.bfloat16), 'row',...  18.8 us
    all_to_all x1, waiting for transfers between devices, on_device(): lax.all_to_all(outbox(own_tokens), 'row', split_axis=0, concat_axis=0, ti...  14.2 us
  transfers between devices with their start and end apart: 17, of which 12 were waited for; matrix products, arithmetic and copies ran while one was open for 19% of the time, Pallas kernels for 0%

profile of v1, /device:TPU:0, one launch (start us, length us, event | category | flops | bytes accessed | tf_op | source)
XLA Modules:
  0.0 498.3 jit_solution(13661178069624658935)
XLA Ops:
  13.7 5.3 %all-to-all-start = ((bf16[8,128,512]{2,1,0:T(8,128)(2,1)}), bf16[8,128,512]{2,1,0:T(8,128)(2,1)S(1)}, u32[]{:S(2)}, u32[]{:S(2)}) async-start(bf16[8,128,512]{2,1,0:T(8,128)(2,1)} %get-tuple-element.40), calls=%async_computation | async-start | bytes 2097152 | tf_op jit(solution)/shard_map/all_to_all | solution.py:74
  20.2 14.2 %all-to-all-done = bf16[8,128,512]{2,1,0:T(8,128)(2,1)S(1)} async-done(((bf16[8,128,512]{2,1,0:T(8,128)(2,1)}), bf16[8,128,512]{2,1,0:T(8,128)(2,1)S(1)}, u32[]{:S(2)}, u32[]{:S(2)}) %all-to-all-start) | async-done | bytes 1048608 | tf_op jit(solution)/shard_map/all_to_all | solution.py:74
  34.4 4.2 all-to-all-start.1
  42.5 11.6 %all-to-all-done.1 = bf16[8,128,512]{2,1,0:T(8,128)(2,1)} async-done(((bf16[8,128,512]{2,1,0:T(8,128)(2,1)}), bf16[8,128,512]{2,1,0:T(8,128)(2,1)}, u32[]{:S(2)}, u32[]{:S(2)}) %all-to-all-start.1) | async-done | bytes 1048608 | tf_op jit(solution)/shard_map/all_to_all | solution.py:75
  61.5 15.1 %collective-permute-done = bf16[256,2048]{1,0:T(8,128)(2,1)S(1)} collective-permute-done((bf16[256,2048]{1,0:T(8,128)(2,1)S(1)}, bf16[256,2048]{1,0:T(8,128)(2,1)S(1)}, u32[]{:S(2)}, u32[]{:S(2)}) %collective-permute-start) | collective-permute-done | bytes 1048608 | tf_op jit(solution)/shard_map/ppermute | solution.py:102
  76.6 15.1 %collective-permute-done.1 = bf16[256,2048]{1,0:T(8,128)(2,1)S(1)} collective-permute-done((bf16[256,2048]{1,0:T(8,128)(2,1)S(1)}, bf16[256,2048]{1,0:T(8,128)(2,1)S(1)}, u32[]{:S(2)}, u32[]{:S(2)}) %collective-permute-start.1) | collective-permute-done | bytes 1048608 | tf_op jit(solution)/shard_map/ppermute | solution.py:102
  92.7 15.1 %collective-permute-done.2 = bf16[256,2048]{1,0:T(8,128)(2,1)S(1)} collective-permute-done((bf16[256,2048]{1,0:T(8,128)(2,1)S(1)}, bf16[256,2048]{1,0:T(8,128)(2,1)S(1)}, u32[]{:S(2)}, u32[]{:S(2)}) %collective-permute-start.2) | collective-permute-done | bytes 1048608 | tf_op jit(solution)/shard_map/ppermute | solution.py:102
  108.8 26.5 %collective-permute-done.3 = bf16[256,2048]{1,0:T(8,128)(2,1)} collective-permute-done((bf16[256,2048]{1,0:T(8,128)(2,1)S(1)}, bf16[256,2048]{1,0:T(8,128)(2,1)}, u32[]{:S(2)}, u32[]{:S(2)}) %collective-permute-start.3) | collective-permute-done | bytes 1048608 | tf_op jit(solution)/shard_map/ppermute | solution.py:102
  138.5 3.9 all-to-all-start.3
  142.4 25.7 %collective-permute-done.4 = bf16[256,2048]{1,0:T(8,128)(2,1)} collective-permute-done((bf16[256,2048]{1,0:T(8,128)(2,1)}, bf16[256,2048]{1,0:T(8,128)(2,1)}, u32[]{:S(2)}, u32[]{:S(2)}) %collective-permute-start.4) | collective-permute-done | bytes 1048608 | tf_op jit(solution)/shard_map/ppermute | solution.py:102
  169.3 3.9 all-to-all-start.2
  175.3 9.2 %all-to-all-done.2 = bf16[8,1,128]{2,1,0:T(2,128)(2,1)S(1)} async-done(((bf16[8,1,128]{2,1,0:T(2,128)(2,1)}), bf16[8,1,128]{2,1,0:T(2,128)(2,1)S(1)}, u32[]{:S(2)}, u32[]{:S(2)}) %all-to-all-start.2) | async-done | bytes 2080 | tf_op jit(solution)/shard_map/all_to_all | solution.py:76
  185.5 10.8 %fusion.26 = f32[512,2048]{1,0:T(8,128)} fusion(bf16[512,2048]{1,0:T(8,128)(2,1)} %all-gather.5.cloned.1.call-done, bf16[2048,2048]{1,0:T(8,128)(2,1)} %all-gather.7.cloned.1.call-done), kind=kOutput, calls=%fused_computation.95 | convolution fusion | flops 4294967296 | bytes 14680064 | tf_op jit(solution)/shard_map/dot_general | solution.py:106
  196.3 39.9 %all-gather.9.cloned.1.call-done = bf16[2048,2048]{1,0:T(8,128)(2,1)} async-done(((bf16[256,2048]{1,0:T(8,128)(2,1)}), bf16[2048,2048]{1,0:T(8,128)(2,1)}) %all-gather.9.cloned.1.call-update) | async-done | bytes 8388624 | tf_op jit(solution)/shard_map/all_gather | solution.py:99
  236.1 12.7 %multiply_convert_fusion.2 = (bf16[512,2048]{1,0:T(8,128)(2,1)}, f32[512,2048]{1,0:T(8,128)}) fusion(f32[512,2048]{1,0:T(8,128)} %fusion.26, bf16[512,2048]{1,0:T(8,128)(2,1)} %all-gather.5.cloned.1.call-done, bf16[2048,2048]{1,0:T(8,128)(2,1)} %all-gather.9.cloned.1.call-done), kind=kOutput, calls=%fused_computation.14 | convolution fusion | flops 4301258752 | bytes 20971520 | tf_op jit(solution)/shard_map/dot_general | solution.py:107
  248.8 35.0 %all-gather.11.cloned.1.call-done = bf16[512,2048]{1,0:T(8,128)(2,1)} async-done(((bf16[512,512]{1,0:T(8,128)(2,1)}), bf16[512,2048]{1,0:T(8,128)(2,1)}) %all-gather.11.cloned.1.call-update) | async-done | bytes 2097168 | tf_op jit(solution)/shard_map/all_gather | solution.py:95
  283.8 10.1 %divide_convert_fusion = bf16[2048,2048]{0,1:T(8,128)(2,1)} fusion(f32[]{:T(128)S(6)} %add.113, bf16[512,2048]{1,0:T(8,128)(2,1)} %get-tuple-element.43, bf16[512,2048]{1,0:T(8,128)(2,1)} %all-gather.11.cloned.1.call-done, bf16[512]{0:T(512)(128)(2,1)S(1)} %get-tuple-element.29), kind=kOutput, calls=%fused_computation.7 | convolution fusion | flops 4304404480 | bytes 12583940 | tf_op jit(solution)/shard_map/dot_general | solution.py:22
  307.8 6.1 %fusion = f32[512,2048]{1,0:T(8,128)} fusion(bf16[512,2048]{1,0:T(8,128)(2,1)S(1)} %copy-done.9, bf16[4096,2048]{1,0:T(8,128)(2,1)S(1)} %constant_dynamic-update-slice_fusion, s32[]{:T(128)S(6)} %select_n.137), kind=kOutput, calls=%fused_computation.10 | convolution fusion | flops 4294967296 | bytes 14680068 | tf_op jit(solution)/shard_map/dot_general | solution.py:108
  314.0 8.8 %divide_convert_fusion.2 = bf16[2048,2048]{0,1:T(8,128)(2,1)S(1)} fusion(f32[]{:T(128)S(6)} %add.113, bf16[512,2048]{1,0:T(8,128)(2,1)S(1)} %copy-done.8, f32[512,2048]{1,0:T(8,128)} %fusion.26, f32[512,2048]{1,0:T(8,128)} %get-tuple-element.44, f32[512,2048]{1,0:T(8,128)} %fusion, f32[512]{0:T(512)S(1)} %get-tuple-element.28), kind=kOutput, calls=%fused_computation.9 | convolution fusion | flops 4314890240 | bytes 23070724 | tf_op jit(solution)/shard_map/dot_general | solution.py:22
  322.8 11.9 %divide_convert_fusion.1 = bf16[2048,2048]{0,1:T(8,128)(2,1)} fusion(f32[]{:T(128)S(6)} %add.113, bf16[512,2048]{1,0:T(8,128)(2,1)S(1)} %copy-done.8, f32[512,2048]{1,0:T(8,128)} %fusion, f32[512]{0:T(512)S(1)} %get-tuple-element.28, f32[512,2048]{1,0:T(8,128)} %fusion.26), kind=kOutput, calls=%fused_computation.8 | convolution fusion | flops 4310695936 | bytes 18876420 | tf_op jit(solution)/shard_map/dot_general | solution.py:22
  334.7 10.6 %pad_maximum_fusion = bf16[2048,4096]{0,1:T(8,128)(2,1)} fusion(bf16[2048,2048]{0,1:T(8,128)(2,1)} %divide_convert_fusion.1, bf16[2048,2048]{0,1:T(8,128)(2,1)S(1)} %divide_convert_fusion.2), kind=kLoop, calls=%fused_computation.6 | loop fusion | flops 33554432 | bytes 33554432 | tf_op jit(solution)/shard_map/concatenate | solution.py:120
  345.4 18.8 %reduce-scatter.5.cloned.1.call-done = bf16[256,2048]{0,1:T(8,128)(2,1)} async-done(((bf16[2048,2048]{0,1:T(8,128)(2,1)}), bf16[256,2048]{0,1:T(8,128)(2,1)}) %reduce-scatter.5.cloned.1.call-update) | async-done | bytes 1048592 | tf_op jit(solution)/shard_map/reduce_scatter | solution.py:116
  366.7 116.9 %reduce-scatter.3.cloned.1.call-done = bf16[256,4096]{0,1:T(8,128)(2,1)} async-done(((bf16[2048,4096]{0,1:T(8,128)(2,1)}), bf16[256,4096]{0,1:T(8,128)(2,1)}) %reduce-scatter.3.cloned.1.call-update) | async-done | bytes 2097168 | tf_op jit(solution)/shard_map/reduce_scatter | solution.py:119
  483.6 3.2 fusion.24
  (114 shorter events, 46.7 us)
Async XLA Ops:
  12.1 26.9 %copy-start = (bf16[768,512]{1,0:T(8,128)(2,1)S(1)}, bf16[768,512]{1,0:T(8,128)(2,1)}, u32[]{:S(2)}) copy-start(bf16[768,512]{1,0:T(8,128)(2,1)} %param.12) | copy-start | bytes 2359300
  13.7 40.4 %copy-start.1 = (bf16[768,512]{1,0:T(8,128)(2,1)S(1)}, bf16[768,512]{1,0:T(8,128)(2,1)}, u32[]{:S(2)}) copy-start(bf16[768,512]{1,0:T(8,128)(2,1)} %param.13) | copy-start | bytes 2359300
  13.7 20.7 %all-to-all-start = ((bf16[8,128,512]{2,1,0:T(8,128)(2,1)}), bf16[8,128,512]{2,1,0:T(8,128)(2,1)S(1)}, u32[]{:S(2)}, u32[]{:S(2)}) async-start(bf16[8,128,512]{2,1,0:T(8,128)(2,1)} %get-tuple-element.40), calls=%async_computation | async-start | bytes 2097152 | tf_op jit(solution)/shard_map/all_to_all | solution.py:74
  34.4 19.6 %all-to-all-start.1 = ((bf16[8,128,512]{2,1,0:T(8,128)(2,1)}), bf16[8,128,512]{2,1,0:T(8,128)(2,1)}, u32[]{:S(2)}, u32[]{:S(2)}) async-start(bf16[8,128,512]{2,1,0:T(8,128)(2,1)} %get-tuple-element.39), calls=%async_computation.1 | async-start | bytes 2097152 | tf_op jit(solution)/shard_map/all_to_all | solution.py:75
  38.7 146.8 %all-gather.5.cloned.1.call-start = ((), (), s32[]{:S(2)}) async-start(), calls=%async_computation.6 | async-start | bytes 2621440 | tf_op jit(solution)/shard_map/all_gather | solution.py:94
  42.4 19.0 %copy-start.2 = (bf16[256,2048]{1,0:T(8,128)(2,1)S(1)}, bf16[256,2048]{1,0:T(8,128)(2,1)}, u32[]{:S(2)}) copy-start(bf16[256,2048]{1,0:T(8,128)(2,1)} %param.19) | copy-start | bytes 3145732
  42.4 92.8 %copy-start.7 = (s32[768]{0:T(1024)S(1)}, s32[768]{0:T(1024)}, u32[]{:S(2)}) copy-start(s32[768]{0:T(1024)} %param.16) | copy-start | bytes 9220
  59.9 125.6 %all-gather.7.cloned.1.call-start = ((), (), s32[]{:S(2)}) async-start(), calls=%async_computation.7 | async-start | bytes 9437184 | tf_op jit(solution)/shard_map/all_gather | solution.py:98
  60.7 175.4 %all-gather.9.cloned.1.call-start = ((), (), s32[]{:S(2)}) async-start(), calls=%async_computation.8 | async-start | bytes 9437184 | tf_op jit(solution)/shard_map/all_gather | solution.py:99
  61.4 15.2 %collective-permute-start = (bf16[256,2048]{1,0:T(8,128)(2,1)S(1)}, bf16[256,2048]{1,0:T(8,128)(2,1)S(1)}, u32[]{:S(2)}, u32[]{:S(2)}) collective-permute-start(bf16[256,2048]{1,0:T(8,128)(2,1)S(1)} %copy-done.2), channel_id=1, source_target_pairs={{0,4},{4,8},{8,12},{12,16},{16,20},{20,24},{24,28},{28,0},{1,5},{5... | collective-permute-start | bytes 3145736 | tf_op jit(solution)/shard_map/ppermute | solution.py:102
  76.6 15.1 %collective-permute-start.1 = (bf16[256,2048]{1,0:T(8,128)(2,1)S(1)}, bf16[256,2048]{1,0:T(8,128)(2,1)S(1)}, u32[]{:S(2)}, u32[]{:S(2)}) collective-permute-start(bf16[256,2048]{1,0:T(8,128)(2,1)S(1)} %collective-permute-done), channel_id=1, source_target_pairs={{0,4},{4,8},{8,12},{12,16},{16,20},{20,24},{24,28},{28,0},{1,5},{5... | collective-permute-start | bytes 3145736 | tf_op jit(solution)/shard_map/ppermute | solution.py:102
  92.7 15.1 %collective-permute-start.2 = (bf16[256,2048]{1,0:T(8,128)(2,1)S(1)}, bf16[256,2048]{1,0:T(8,128)(2,1)S(1)}, u32[]{:S(2)}, u32[]{:S(2)}) collective-permute-start(bf16[256,2048]{1,0:T(8,128)(2,1)S(1)} %collective-permute-done.1), channel_id=1, source_target_pairs={{0,4},{4,8},{8,12},{12,16},{16,20},{20,24},{24,28},{28,0},{1,5},{5... | collective-permute-start | bytes 3145736 | tf_op jit(solution)/shard_map/ppermute | solution.py:102
  108.8 26.5 %collective-permute-start.3 = (bf16[256,2048]{1,0:T(8,128)(2,1)S(1)}, bf16[256,2048]{1,0:T(8,128)(2,1)}, u32[]{:S(2)}, u32[]{:S(2)}) collective-permute-start(bf16[256,2048]{1,0:T(8,128)(2,1)S(1)} %collective-permute-done.2), channel_id=1, source_target_pairs={{0,4},{4,8},{8,12},{12,16},{16,20},{20,24},{24,28},{28,0},{1,5},{5... | collective-permute-start | bytes 3145736 | tf_op jit(solution)/shard_map/ppermute | solution.py:102
  135.2 32.9 %collective-permute-start.4 = (bf16[256,2048]{1,0:T(8,128)(2,1)}, bf16[256,2048]{1,0:T(8,128)(2,1)}, u32[]{:S(2)}, u32[]{:S(2)}) collective-permute-start(bf16[256,2048]{1,0:T(8,128)(2,1)} %collective-permute-done.3), channel_id=1, source_target_pairs={{0,4},{4,8},{8,12},{12,16},{16,20},{20,24},{24,28},{28,0},{1,5},{5... | collective-permute-start | bytes 3145736 | tf_op jit(solution)/shard_map/ppermute | solution.py:102
  138.5 30.8 %all-to-all-start.3 = ((bf16[8,1,2]{2,1,0:T(2,128)(2,1)}), bf16[8,1,2]{2,1,0:T(2,128)(2,1)S(1)}, u32[]{:S(2)}, u32[]{:S(2)}) async-start(bf16[8,1,2]{2,1,0:T(2,128)(2,1)} %broadcast_in_dim.133), calls=%async_computation.3 | async-start | bytes 8192 | tf_op jit(solution)/shard_map/all_to_all | solution.py:77
  168.1 17.1 %collective-permute-start.5 = (bf16[256,2048]{1,0:T(8,128)(2,1)}, bf16[256,2048]{1,0:T(8,128)(2,1)}, u32[]{:S(2)}, u32[]{:S(2)}) collective-permute-start(bf16[256,2048]{1,0:T(8,128)(2,1)} %collective-permute-done.4), channel_id=1, source_target_pairs={{0,4},{4,8},{8,12},{12,16},{16,20},{20,24},{24,28},{28,0},{1,5},{5... | collective-permute-start | bytes 3145736 | tf_op jit(solution)/shard_map/ppermute | solution.py:102
  169.3 15.1 %all-to-all-start.2 = ((bf16[8,1,128]{2,1,0:T(2,128)(2,1)}), bf16[8,1,128]{2,1,0:T(2,128)(2,1)S(1)}, u32[]{:S(2)}, u32[]{:S(2)}) async-start(bf16[8,1,128]{2,1,0:T(2,128)(2,1)} %copy.44), calls=%async_computation.2 | async-start | bytes 8192 | tf_op jit(solution)/shard_map/all_to_all | solution.py:76
  173.3 110.5 %all-gather.11.cloned.1.call-start = ((), (), s32[]{:S(2)}) async-start(), calls=%async_computation.9 | async-start | bytes 2621440 | tf_op jit(solution)/shard_map/all_gather | solution.py:95
  185.1 179.1 %reduce-scatter.5.cloned.1.call-start = ((), (), s32[]{:S(2)}) async-start(), calls=%async_computation.11 | async-start | bytes 9437184 | tf_op jit(solution)/shard_map/reduce_scatter | solution.py:116
  185.2 109.0 %collective-permute-start.6 = (bf16[256,2048]{1,0:T(8,128)(2,1)}, bf16[256,2048]{1,0:T(8,128)(2,1)}, u32[]{:S(2)}, u32[]{:S(2)}) collective-permute-start(bf16[256,2048]{1,0:T(8,128)(2,1)} %collective-permute-done.5), channel_id=1, source_target_pairs={{0,4},{4,8},{8,12},{12,16},{16,20},{20,24},{24,28},{28,0},{1,5},{5... | collective-permute-start | bytes 3145736 | tf_op jit(solution)/shard_map/ppermute | solution.py:102
  293.9 189.7 %reduce-scatter.3.cloned.1.call-start = ((), (), s32[]{:S(2)}) async-start(), calls=%async_computation.10 | async-start | bytes 18874368 | tf_op jit(solution)/shard_map/reduce_scatter | solution.py:119
  294.2 5.5 %copy-start.6 = (bf16[256,2048]{1,0:T(8,128)(2,1)S(1)}, bf16[256,2048]{1,0:T(8,128)(2,1)}, u32[]{:S(2)}) copy-start(bf16[256,2048]{1,0:T(8,128)(2,1)} %copy-done.5) | copy-start | bytes 3145732
  295.6 4.2 copy-start.4
  307.8 6.1 %copy-start.8 = (bf16[512,2048]{1,0:T(8,128)(2,1)S(1)}, bf16[512,2048]{1,0:T(8,128)(2,1)}, u32[]{:S(2)}) copy-start(bf16[512,2048]{1,0:T(8,128)(2,1)} %all-gather.5.cloned.1.call-done) | copy-start | bytes 6291460
  (3 other events, 3.9 us)
Sparse Core Ops, SparseCore 0:
  60.0 45.0 all-gather.4
  107.0 68.4 all-gather.6
  177.4 58.6 all-gather.8
  238.1 45.6 all-gather.10
  294.0 70.0 reduce-scatter.4
  367.6 116.0 reduce-scatter.2
